TPU v7x, 128 devices: a whole 4x4x4 slice. The times are simulated.
128 devices in a mesh: gx: 4 (over y), gy: 8 (over z, x_lo), gz: 4 (over x_hi, core).
Axes of the slice: x: 4 (x_hi: 2, x_lo: 2; x = x_hi * 2 + x_lo), y: 4, z: 4, core: 2. Of those that a mesh axis runs over, the one named last changes fastest.
Arguments:
- node_latent: bfloat16 [64, 256, 16, 128], P('gx', 'gy', 'gz'), may hold values from -6 to 6
- edge_latent: bfloat16 [4, 8, 4, 12288, 128], P('gx', 'gy', 'gz'), may hold values from -6 to 6
- senders: int32 [4, 8, 4, 12288], P('gx', 'gy', 'gz'), may hold values from 7 to 3664, as said below
- receivers: int32 [4, 8, 4, 12288], P('gx', 'gy', 'gz'), may hold values from 0 to 2047, as said below
- w1_edge: bfloat16 [384, 128], replicated, may hold values from -0.3125 to 0.3125
- b1_edge: float32 [128], replicated, may hold values from -3 to 3
- w2_edge: bfloat16 [128, 128], replicated, may hold values from -0.5 to 0.5
- b2_edge: float32 [128], replicated, may hold values from -3 to 3
- w1_node: bfloat16 [256, 128], replicated, may hold values from -0.375 to 0.375
- b1_node: float32 [128], replicated, may hold values from -3 to 3
- w2_node: bfloat16 [128, 128], replicated, may hold values from -0.5 to 0.5
- cot_node: bfloat16 [64, 256, 16, 128], P('gx', 'gy', 'gz'), may hold values from -6 to 6
- cot_edge: bfloat16 [4, 8, 4, 12288, 128], P('gx', 'gy', 'gz'), may hold values from -8 to 8
Outputs:
- grad_node: bfloat16 [64, 256, 16, 128], P('gx', 'gy', 'gz')
- grad_edge: bfloat16 [4, 8, 4, 12288, 128], P('gx', 'gy', 'gz')
- grad_w1_edge: float32 [384, 128], replicated
- grad_w2_edge: float32 [128, 128], replicated
- grad_w1_node: float32 [256, 128], replicated
- grad_w2_node: float32 [128, 128], replicated
- grad_biases: float32 [4, 128], replicated
Inputs may be any that keep to these rules, and one draw needn't show every extreme that they name: `receivers`: in every block the list is nondecreasing; entry (i * 32 + j) * 4 + l names the block's cell at local coordinates (i, j, l). `senders`: entry (p * 34 + q) * 6 + r names the cell at local coordinates (p - 1, q - 1, r - 1) of the block extended by one cell on every side, the extension being cells of the adjacent blocks around the periodic box; it is always one of the six face neighbours of the same slot's receiver.
All inputs are finite; a program needn't handle non-finite values.
Results may differ from a plain program's by a relative error of at most 0.01.
Values may be sent and summed in bfloat16 or wider, within the bound.
A program may use at most 128 MiB of HBM per device.

v0:
```python
import jax
import jax.numpy as jnp
from jax import lax
from jax.sharding import PartitionSpec as P


def with_halo(shard, sides, width):
    edges = {}
    for axis, dim in sides:
        peers, length = (lax.axis_size(axis), shard.shape[dim])
        up = [(i, (i + 1) % peers) for i in range(peers)]
        last = lax.slice_in_dim(shard, length - width, length, axis=dim)
        leading = lax.slice_in_dim(shard, 0, width, axis=dim)
        edges[dim] = (
            lax.ppermute(last, axis, up),
            lax.ppermute(leading, axis, [(b, a) for a, b in up]),
        )
    done = []
    for _, dim in sides:
        low, high = edges[dim]
        around = [(width, width) if d in done else (0, 0) for d in range(shard.ndim)]
        shard = jnp.concatenate([jnp.pad(low, around), shard, jnp.pad(high, around)], axis=dim)
        done.append(dim)
    return shard


def transposed_dot(left, right):
    return lax.dot_general(
        left, right, (((0,), (0,)), ((), ())), preferred_element_type=jnp.float32
    )


def column_sums(values):
    return jnp.sum(values.astype(jnp.float32), axis=0)


def silu_slope(values):
    sigma = jax.nn.sigmoid(values)
    return sigma * (1.0 + values * (1.0 - sigma))


def reduce_flat(flat_grads):
    return lax.psum(flat_grads, ("gx", "gy", "gz"))


def on_device(
    node_latent,
    edge_latent,
    senders,
    receivers,
    w1_edge,
    b1_edge,
    w2_edge,
    b2_edge,
    w1_node,
    b1_node,
    w2_node,
    cot_node,
    cot_edge,
):
    side_x, side_y, side_z, latent = node_latent.shape
    cell_count = side_x * side_y * side_z
    edge_count = edge_latent.shape[3]
    padded = with_halo(node_latent, (("gx", 0), ("gy", 1), ("gz", 2)), 1)
    flat_pad = padded.reshape(-1, latent)
    own_rows = node_latent.reshape(cell_count, latent)
    edge_rows = edge_latent.reshape(edge_count, latent)
    cot_rows = cot_edge.reshape(edge_count, latent)
    cot_cells = cot_node.reshape(cell_count, latent)
    sender_ids = senders.reshape(edge_count)
    receiver_ids = receivers.reshape(edge_count)
    sender_rows = jnp.take(flat_pad, sender_ids, axis=0)
    receiver_rows = jnp.take(own_rows, receiver_ids, axis=0)
    x_edge = jnp.concatenate([edge_rows, sender_rows, receiver_rows], axis=1)
    z_edge = jnp.dot(x_edge, w1_edge, preferred_element_type=jnp.float32) + b1_edge
    u_edge = jax.nn.silu(z_edge).astype(jnp.bfloat16)
    edge_new = (
        edge_rows.astype(jnp.float32)
        + jnp.dot(u_edge, w2_edge, preferred_element_type=jnp.float32)
        + b2_edge
    ).astype(jnp.bfloat16)
    aggregate = jax.ops.segment_sum(
        edge_new.astype(jnp.float32), receiver_ids, cell_count, indices_are_sorted=True
    ).astype(jnp.bfloat16)
    x_node = jnp.concatenate([own_rows, aggregate], axis=1)
    z_node = jnp.dot(x_node, w1_node, preferred_element_type=jnp.float32) + b1_node
    u_node = jax.nn.silu(z_node).astype(jnp.bfloat16)
    dz_node = (
        jnp.dot(cot_cells, w2_node.T, preferred_element_type=jnp.float32) * silu_slope(z_node)
    ).astype(jnp.bfloat16)
    dx_node = jnp.dot(dz_node, w1_node.T, preferred_element_type=jnp.float32)
    node_flat = jnp.concatenate(
        [
            transposed_dot(x_node, dz_node).reshape(-1),
            column_sums(dz_node),
            transposed_dot(u_node, cot_cells).reshape(-1),
            column_sums(cot_cells),
        ]
    )
    d_edge = (
        cot_rows.astype(jnp.float32) + jnp.take(dx_node[:, latent:], receiver_ids, axis=0)
    ).astype(jnp.bfloat16)
    dz_edge = (
        jnp.dot(d_edge, w2_edge.T, preferred_element_type=jnp.float32) * silu_slope(z_edge)
    ).astype(jnp.bfloat16)
    d_self = jnp.dot(dz_edge, w1_edge[:latent].T, preferred_element_type=jnp.float32)
    d_sender = jnp.dot(dz_edge, w1_edge[latent : 2 * latent].T, preferred_element_type=jnp.float32)
    d_receiver = jnp.dot(dz_edge, w1_edge[2 * latent :].T, preferred_element_type=jnp.float32)
    grad_edge = (
        (d_edge.astype(jnp.float32) + d_self).astype(jnp.bfloat16).reshape(edge_latent.shape)
    )
    edge_flat = jnp.concatenate(
        [
            transposed_dot(x_edge, dz_edge).reshape(-1),
            column_sums(dz_edge),
            transposed_dot(u_edge, d_edge).reshape(-1),
            column_sums(d_edge),
        ]
    )
    summed = (reduce_flat(jnp.concatenate([node_flat, edge_flat])),)
    send_grid = jax.ops.segment_sum(d_sender, sender_ids, flat_pad.shape[0]).reshape(
        side_x + 2, side_y + 2, side_z + 2, latent
    )
    receiver_sum = jax.ops.segment_sum(
        d_receiver, receiver_ids, cell_count, indices_are_sorted=True
    )
    own_terms = cot_cells.astype(jnp.float32) + dx_node[:, :latent] + receiver_sum
    interior = send_grid[1:-1, 1:-1, 1:-1] + own_terms.reshape(side_x, side_y, side_z, latent)
    extended = with_halo(
        send_grid.astype(jnp.bfloat16), (("gx", 0), ("gy", 1), ("gz", 2)), 1
    ).astype(send_grid.dtype)
    interior = interior.at[0].add(extended[0, 2:-2, 2:-2]).at[-1].add(extended[-1, 2:-2, 2:-2])
    interior = (
        interior.at[:, 0].add(extended[2:-2, 0, 2:-2]).at[:, -1].add(extended[2:-2, -1, 2:-2])
    )
    interior = (
        interior.at[:, :, 0].add(extended[2:-2, 2:-2, 0]).at[:, :, -1].add(extended[2:-2, 2:-2, -1])
    )
    grad_node = interior.astype(jnp.bfloat16)
    param_count = 7 * latent * latent + 4 * latent
    partial_value = sum((jnp.sum(portion * portion) for portion in summed))
    factor = 1.0 / jnp.maximum(1.0, jnp.sqrt(partial_value / param_count))
    scaled = [portion * factor for portion in summed]
    full_grads = scaled[0]
    square = latent * latent
    cut_a = 2 * square
    cut_b = cut_a + latent
    cut_c = cut_b + square
    cut_d = cut_c + latent
    cut_e = cut_d + 3 * square
    cut_f = cut_e + latent
    cut_g = cut_f + square
    grad_w1_node = full_grads[:cut_a].reshape(2 * latent, latent)
    bias_one_node = full_grads[cut_a:cut_b]
    grad_w2_node = full_grads[cut_b:cut_c].reshape(latent, latent)
    bias_two_node = full_grads[cut_c:cut_d]
    grad_w1_edge = full_grads[cut_d:cut_e].reshape(3 * latent, latent)
    bias_one_edge = full_grads[cut_e:cut_f]
    grad_w2_edge = full_grads[cut_f:cut_g].reshape(latent, latent)
    bias_two_edge = full_grads[cut_g:]
    grad_biases = jnp.stack([bias_one_edge, bias_two_edge, bias_one_node, bias_two_node])
    return (
        grad_node,
        grad_edge,
        grad_w1_edge,
        grad_w2_edge,
        grad_w1_node,
        grad_w2_node,
        grad_biases,
    )


def solution(mesh):
    placed = (
        P("gx", "gy", "gz", None),
        P("gx", "gy", "gz", None, None),
        P("gx", "gy", "gz", None),
        P("gx", "gy", "gz", None),
        P(),
        P(),
        P(),
        P(),
        P(),
        P(),
        P(),
        P("gx", "gy", "gz", None),
        P("gx", "gy", "gz", None, None),
    )
    return jax.shard_map(
        on_device,
        mesh=mesh,
        in_specs=placed,
        out_specs=(
            P("gx", "gy", "gz", None),
            P("gx", "gy", "gz", None, None),
            P(),
            P(),
            P(),
            P(),
            P(),
        ),
        check_vma=False,
    )
```

profile of v0, /device:TPU:1, one launch (start us, length us, event | category | flops | bytes accessed | tf_op | source)
XLA Modules:
  0.0 521.8 jit_solution(16961521660698633385)
XLA Ops:
  10.2 3.6 collective-permute-start.4
  19.2 3.8 collective-permute-start
  28.0 43.3 %gather_fusion.1 = bf16[12288,128]{1,0:T(8,128)(2,1)} fusion(bf16[2048,128]{1,0:T(8,128)(2,1)S(1)} %bitcast.62, s32[12288]{0:T(1024)S(1)} %broadcast_clamp_fusion), kind=kCustom, calls=%fused_computation.1 | custom fusion | bytes 6340608 | tf_op jit(solution)/shard_map/jit(_take)/gather | solution.py:73
  73.8 43.7 %gather_fusion = bf16[12288,128]{1,0:T(8,128)(2,1)} fusion(bf16[3672,128]{1,0:T(8,128)(2,1)S(1)} %reshape.366, s32[12288]{0:T(1024)S(1)} %broadcast_clamp_fusion.1), kind=kCustom, calls=%fused_computation | custom fusion | bytes 6340608 | tf_op jit(solution)/shard_map/jit(_take)/gather | solution.py:72
  117.5 9.2 %broadcast_select_fusion = (bf16[12288,128]{1,0:T(8,128)(2,1)S(1)}, bf16[12288,128]{1,0:T(8,128)(2,1)S(1)}) fusion(bf16[12288,128]{1,0:T(8,128)(2,1)} %gather_fusion, pred[12288]{0:T(1024)(128)(4,1)S(1)} %compare_and_fusion, bf16[12288,128]{1,0:T(8,128)(2,1)} %gather_fusion.1, pred[12288]{0:T(1024)(128)(4,1)S(1)} %compare_and_fusion.1), kind=kLoop, calls=%fused_computation.38 | loop fusion | flops 3145728 | bytes 12607488 | tf_op jit(solution)/shard_map/jit(_take)/select_n | solution.py:72
  126.8 3.0 convolution_add_fusion.2
  132.5 3.8 fusion.4
  136.3 76.0 %scatter_custom_fusion = f32[2048,128]{1,0:T(8,128)S(1)} fusion(s32[12288]{0:T(1024)S(1)} %bitcast.69, f32[12288,128]{1,0:T(8,128)} %fusion.4, f32[]{:T(128)} %constant.207.clone.1), kind=kCustom, calls=%fused_computation.83 | custom fusion | flops 1572864 | bytes 1049088 | tf_op jit(solution)/shard_map/scatter-add | solution.py:82
  215.6 41.2 %gather_fusion.2 = f32[12288,128]{1,0:T(8,128)} fusion(f32[2048,128]{1,0:T(8,128)S(1)} %get-tuple-element.81, s32[12288]{0:T(1024)S(1)} %broadcast_clamp_fusion), kind=kCustom, calls=%fused_computation.2 | custom fusion | bytes 12632064 | tf_op jit(solution)/shard_map/jit(_take)/gather | solution.py:101
  256.8 9.3 %convert_reduce_fusion = (f32[128]{0:T(128)S(1)}, bf16[12288,128]{1,0:T(8,128)(2,1)S(1)}) fusion(f32[12288,128]{1,0:T(8,128)} %gather_fusion.2, pred[12288]{0:T(1024)(128)(4,1)S(1)} %compare_and_fusion.1, bf16[1,1,1,12288,128]{4,3,2,1,0:T(8,128)(2,1)} %param.37), kind=kLoop, calls=%fused_computation.17 | loop fusion | flops 9437056 | bytes 12595712 | tf_op jit(solution)/shard_map/reduce_sum | solution.py:34
  266.1 5.4 %convolution_bitcast_fusion.2 = f32[16384]{0:T(1024)} fusion(bf16[12288,128]{1,0:T(8,128)(2,1)S(1)} %get-tuple-element.80, f32[12288,128]{1,0:T(8,128)} %copy-done.25), kind=kOutput, calls=%fused_computation.63 | convolution fusion | flops 410517504 | bytes 9502720 | tf_op jit(solution)/shard_map/dot_general | solution.py:28
  271.6 3.2 convert_reduce_fusion.1
  275.3 3.3 convolution_bitcast_fusion
  281.3 3.6 fusion.47
  284.9 3.6 fusion.49
  288.5 66.6 %scatter_custom_fusion.1 = f32[3672,128]{1,0:T(8,128)S(1)} fusion(s32[12288]{0:T(1024)} %bitcast.74, f32[12288,128]{1,0:T(8,128)} %fusion.49, f32[]{:T(128)} %constant.207.clone.1), kind=kCustom, calls=%fused_computation.81 | custom fusion | flops 1572864 | bytes 1880576 | tf_op jit(solution)/shard_map/scatter-add | solution.py:121
  361.8 3.6 collective-permute-start.10
  368.1 4.4 collective-permute-start.6
  372.5 76.1 %scatter_fusion = f32[2048,128]{1,0:T(8,128)S(1)} fusion(f32[2048,128]{1,0:T(8,128)S(1)} %get-tuple-element.82, s32[12288]{0:T(1024)S(1)} %bitcast.70, f32[12288,128]{1,0:T(8,128)} %fusion.47), kind=kCustom, calls=%fused_computation.5 | custom fusion | flops 1572864 | bytes 18923520 | tf_op jit(solution)/shard_map/scatter-add | solution.py:124
  451.4 5.5 %collective-permute-done.11 = bf16[18,34,1,128]{3,2,1,0:T(2,128)(2,1)S(1)} collective-permute-done((bf16[18,34,1,128]{3,2,1,0:T(2,128)(2,1)}, bf16[18,34,1,128]{3,2,1,0:T(2,128)(2,1)S(1)}, u32[]{:S(2)}, u32[]{:S(2)}) %collective-permute-start.11) | collective-permute-done | bytes 156704 | tf_op jit(solution)/shard_map/ppermute | solution.py:16
  456.8 3.4 fusion.30
  462.2 5.3 %scatter-add.58 = f32[16,32,4,128]{3,2,1,0:T(4,128)S(1)} dynamic-update-slice(f32[16,32,4,128]{3,2,1,0:T(4,128)S(1)} %fusion.44, f32[16,32,1,128]{3,2,1,0:T(1,128)S(1)} %slice_add_fusion.3, s32[]{:T(128)} %constant.208.clone.1, s32[]{:T(128)} %constant.208.clone.1, s32[]{:T(128)} %constant.208.clone.1, s32[]{:T(128)} %constant.208.clone.1) | dynamic-update-slice | bytes 524292 | tf_op jit(solution)/shard_map/scatter-add | solution.py:137
  469.5 5.3 %scatter-add.59 = f32[16,32,4,128]{3,2,1,0:T(4,128)S(1)} dynamic-update-slice(f32[16,32,4,128]{3,2,1,0:T(4,128)S(1)} %scatter-add.58, f32[16,32,1,128]{3,2,1,0:T(1,128)S(1)} %slice_add_fusion.2, s32[]{:T(128)} %constant.208.clone.1, s32[]{:T(128)} %constant.208.clone.1, s32[]{:T(128)} %constant.219.clone.1, s32[]{:T(128)} %constant.208.clone.1) | dynamic-update-slice | bytes 524292 | tf_op jit(solution)/shard_map/scatter-add | solution.py:137
  475.8 33.0 %all-reduce.10.cloned.1.call-done = f32[115200]{0:T(1024)} async-done(((f32[115200]{0:T(1024)}), f32[115200]{0:T(1024)}) %all-reduce.10.cloned.1.call-update) | async-done | bytes 460816 | tf_op jit(solution)/shard_map/psum | solution.py:43
  (125 shorter events, 47.1 us)
Async XLA Ops:
  7.2 205.2 %copy-start = (bf16[256,128]{1,0:T(8,128)(2,1)S(1)}, bf16[256,128]{1,0:T(8,128)(2,1)}, u32[]{:S(2)}) copy-start(bf16[256,128]{1,0:T(8,128)(2,1)} %param.33) | copy-start | bytes 196612
  7.2 20.8 %copy-start.2 = (bf16[16,32,4,128]{3,2,1,0:T(4,128)(2,1)S(1)}, bf16[16,32,4,128]{3,2,1,0:T(4,128)(2,1)}, u32[]{:S(2)}) copy-start(bf16[16,32,4,128]{3,2,1,0:T(4,128)(2,1)} %param.25) | copy-start | bytes 1572868
  7.2 501.6 %all-reduce.10.cloned.1.call-start = ((), (), s32[]{:S(2)}) async-start(), calls=%async_computation | async-start | bytes 925696 | tf_op jit(solution)/shard_map/psum | solution.py:43
  8.1 18.3 %collective-permute-start.1 = (bf16[16,1,4,128]{3,2,1,0:T(4,128)(2,1)S(1)}, bf16[16,1,4,128]{3,2,1,0:T(4,128)(2,1)S(1)}, u32[]{:S(2)}, u32[]{:S(2)}) collective-permute-start(bf16[16,1,4,128]{3,2,1,0:T(4,128)(2,1)S(1)} %get-tuple-element.93), channel_id=1, source_target_pairs={{0,4},{4,8},{8,12},{12,16},{16,20},{20,24},{24,28},{28,0},{1,5},{5... | collective-permute-start | bytes 49160 | tf_op jit(solution)/shard_map/ppermute | solution.py:15
  10.2 61.2 %collective-permute-start.4 = (bf16[16,1,4,128]{3,2,1,0:T(4,128)(2,1)S(1)}, bf16[16,1,4,128]{3,2,1,0:T(4,128)(2,1)S(1)}, u32[]{:S(2)}, u32[]{:S(2)}) collective-permute-start(bf16[16,1,4,128]{3,2,1,0:T(4,128)(2,1)S(1)} %get-tuple-element.94), channel_id=1, source_target_pairs={{4,0},{8,4},{12,8},{16,12},{20,16},{24,20},{28,24},{0,28},{5,1},{9... | collective-permute-start | bytes 49160 | tf_op jit(solution)/shard_map/ppermute | solution.py:16
  14.5 56.8 %collective-permute-start.2 = (bf16[1,32,4,128]{3,2,1,0:T(4,128)(2,1)S(1)}, bf16[1,32,4,128]{3,2,1,0:T(4,128)(2,1)S(1)}, u32[]{:S(2)}, u32[]{:S(2)}) collective-permute-start(bf16[1,32,4,128]{3,2,1,0:T(4,128)(2,1)S(1)} %get-tuple-element.89), channel_id=1, source_target_pairs={{0,32},{32,64},{64,96},{96,0},{1,33},{33,65},{65,97},{97,1},{2,34}... | collective-permute-start | bytes 98312 | tf_op jit(solution)/shard_map/ppermute | solution.py:15
  15.9 55.5 %collective-permute-start.3 = (bf16[1,32,4,128]{3,2,1,0:T(4,128)(2,1)S(1)}, bf16[1,32,4,128]{3,2,1,0:T(4,128)(2,1)S(1)}, u32[]{:S(2)}, u32[]{:S(2)}) collective-permute-start(bf16[1,32,4,128]{3,2,1,0:T(4,128)(2,1)S(1)} %get-tuple-element.90), channel_id=1, source_target_pairs={{32,0},{64,32},{96,64},{0,96},{33,1},{65,33},{97,65},{1,97},{34,2}... | collective-permute-start | bytes 98312 | tf_op jit(solution)/shard_map/ppermute | solution.py:16
  19.2 52.2 %collective-permute-start = (bf16[16,32,1,128]{3,2,1,0:T(2,128)(2,1)S(1)}, bf16[16,32,1,128]{3,2,1,0:T(2,128)(2,1)S(1)}, u32[]{:S(2)}, u32[]{:S(2)}) collective-permute-start(bf16[16,32,1,128]{3,2,1,0:T(2,128)(2,1)S(1)} %get-tuple-element.91), channel_id=1, source_target_pairs={{0,1},{1,2},{2,3},{3,0},{4,5},{5,6},{6,7},{7,4},{8,9},{9,10},{10,1... | collective-permute-start | bytes 393224 | tf_op jit(solution)/shard_map/ppermute | solution.py:15
  26.3 45.0 %collective-permute-start.5 = (bf16[16,32,1,128]{3,2,1,0:T(2,128)(2,1)S(1)}, bf16[16,32,1,128]{3,2,1,0:T(2,128)(2,1)S(1)}, u32[]{:S(2)}, u32[]{:S(2)}) collective-permute-start(bf16[16,32,1,128]{3,2,1,0:T(2,128)(2,1)S(1)} %get-tuple-element.92), channel_id=1, source_target_pairs={{1,0},{2,1},{3,2},{0,3},{5,4},{6,5},{7,6},{4,7},{9,8},{10,9},{11,1... | collective-permute-start | bytes 393224 | tf_op jit(solution)/shard_map/ppermute | solution.py:16
  117.5 9.3 %copy-start.12 = (bf16[384,128]{1,0:T(8,128)(2,1)S(1)}, bf16[384,128]{1,0:T(8,128)(2,1)}, u32[]{:S(2)}) copy-start(bf16[384,128]{1,0:T(8,128)(2,1)} %param.29) | copy-start | bytes 294916
  117.5 9.3 %copy-start.17 = (bf16[1,1,1,12288,128]{4,3,2,1,0:T(8,128)(2,1)S(1)}, bf16[1,1,1,12288,128]{4,3,2,1,0:T(8,128)(2,1)}, u32[]{:S(2)}) copy-start(bf16[1,1,1,12288,128]{4,3,2,1,0:T(8,128)(2,1)} %param.26) | copy-start | bytes 9437188
  117.5 9.3 %copy-start.21 = (f32[128]{0:T(128)S(1)}, f32[128]{0:T(128)}, u32[]{:S(2)}) copy-start(f32[128]{0:T(128)} %param.30) | copy-start | bytes 1540
  126.8 5.7 %copy-start.20 = (bf16[128,128]{1,0:T(8,128)(2,1)S(1)}, bf16[128,128]{1,0:T(8,128)(2,1)}, u32[]{:S(2)}) copy-start(bf16[128,128]{1,0:T(8,128)(2,1)} %param.31) | copy-start | bytes 98308
  132.5 79.9 %copy-start.23 = (f32[128]{0:T(128)S(1)}, f32[128]{0:T(128)}, u32[]{:S(2)}) copy-start(f32[128]{0:T(128)} %param.34) | copy-start | bytes 1540
  136.3 76.6 %copy-start.8 = (bf16[16,32,4,128]{3,2,1,0:T(4,128)(2,1)S(1)}, bf16[16,32,4,128]{3,2,1,0:T(4,128)(2,1)}, u32[]{:S(2)}) copy-start(bf16[16,32,4,128]{3,2,1,0:T(4,128)(2,1)} %param.36) | copy-start | bytes 1572868
  256.8 14.7 %slice-start = ((s8[6291456]{0:T(1024)(128)(4,1)}), s8[4194304]{0:T(1024)(128)(4,1)S(1)}, s32[]{:S(2)}) async-start(s8[6291456]{0:T(1024)(128)(4,1)} %bitcast.77), calls=%async_computation.1 | async-start | bytes 8388608
  360.8 87.9 %collective-permute-start.7 = (bf16[18,1,6,128]{3,2,1,0:T(8,128)(2,1)S(1)}, bf16[18,1,6,128]{3,2,1,0:T(8,128)(2,1)S(1)}, u32[]{:S(2)}, u32[]{:S(2)}) collective-permute-start(bf16[18,1,6,128]{3,2,1,0:T(8,128)(2,1)S(1)} %get-tuple-element.87), channel_id=1, source_target_pairs={{0,4},{4,8},{8,12},{12,16},{16,20},{20,24},{24,28},{28,0},{1,5},{5... | collective-permute-start | bytes 82952 | tf_op jit(solution)/shard_map/ppermute | solution.py:15
  361.8 89.5 %collective-permute-start.10 = (bf16[18,1,6,128]{3,2,1,0:T(8,128)(2,1)S(1)}, bf16[18,1,6,128]{3,2,1,0:T(8,128)(2,1)S(1)}, u32[]{:S(2)}, u32[]{:S(2)}) collective-permute-start(bf16[18,1,6,128]{3,2,1,0:T(8,128)(2,1)S(1)} %get-tuple-element.88), channel_id=1, source_target_pairs={{4,0},{8,4},{12,8},{16,12},{20,16},{24,20},{28,24},{0,28},{5,1},{9... | collective-permute-start | bytes 82952 | tf_op jit(solution)/shard_map/ppermute | solution.py:16
  365.4 85.9 %collective-permute-start.8 = (bf16[1,34,6,128]{3,2,1,0:T(8,128)(2,1)}, bf16[1,34,6,128]{3,2,1,0:T(8,128)(2,1)}, u32[]{:S(2)}, u32[]{:S(2)}) collective-permute-start(bf16[1,34,6,128]{3,2,1,0:T(8,128)(2,1)} %get-tuple-element.83), channel_id=1, source_target_pairs={{0,32},{32,64},{64,96},{96,0},{1,33},{33,65},{65,97},{97,1},{2,34}... | collective-permute-start | bytes 156680 | tf_op jit(solution)/shard_map/ppermute | solution.py:15
  365.5 85.8 %collective-permute-start.9 = (bf16[1,34,6,128]{3,2,1,0:T(8,128)(2,1)}, bf16[1,34,6,128]{3,2,1,0:T(8,128)(2,1)}, u32[]{:S(2)}, u32[]{:S(2)}) collective-permute-start(bf16[1,34,6,128]{3,2,1,0:T(8,128)(2,1)} %get-tuple-element.84), channel_id=1, source_target_pairs={{32,0},{64,32},{96,64},{0,96},{33,1},{65,33},{97,65},{1,97},{34,2}... | collective-permute-start | bytes 156680 | tf_op jit(solution)/shard_map/ppermute | solution.py:16
  368.1 83.3 %collective-permute-start.6 = (bf16[18,34,1,128]{3,2,1,0:T(2,128)(2,1)}, bf16[18,34,1,128]{3,2,1,0:T(2,128)(2,1)}, u32[]{:S(2)}, u32[]{:S(2)}) collective-permute-start(bf16[18,34,1,128]{3,2,1,0:T(2,128)(2,1)} %get-tuple-element.85), channel_id=1, source_target_pairs={{0,1},{1,2},{2,3},{3,0},{4,5},{5,6},{6,7},{7,4},{8,9},{9,10},{10,1... | collective-permute-start | bytes 470024 | tf_op jit(solution)/shard_map/ppermute | solution.py:15
  448.7 8.1 %collective-permute-start.11 = (bf16[18,34,1,128]{3,2,1,0:T(2,128)(2,1)}, bf16[18,34,1,128]{3,2,1,0:T(2,128)(2,1)S(1)}, u32[]{:S(2)}, u32[]{:S(2)}) collective-permute-start(bf16[18,34,1,128]{3,2,1,0:T(2,128)(2,1)} %get-tuple-element.86), channel_id=1, source_target_pairs={{1,0},{2,1},{3,2},{0,3},{5,4},{6,5},{7,6},{4,7},{9,8},{10,9},{11,1... | collective-permute-start | bytes 470024 | tf_op jit(solution)/shard_map/ppermute | solution.py:16
  449.3 7.5 %copy-start.16 = (bf16[18,1,6,128]{3,2,1,0:T(8,128)(2,1)S(1)}, bf16[18,1,6,128]{3,2,1,0:T(8,128)(2,1)}, u32[]{:S(2)}) copy-start(bf16[18,1,6,128]{3,2,1,0:T(8,128)(2,1)} %copy-done.15) | copy-start | bytes 82948
  460.3 54.6 %copy-start.1 = (bf16[256,128]{1,0:T(8,128)(2,1)S(1)}, bf16[256,128]{1,0:T(8,128)(2,1)}, u32[]{:S(2)}) copy-start(bf16[256,128]{1,0:T(8,128)(2,1)} %param.33) | copy-start | bytes 196612
  (17 other events, 54.6 us)
Sparse Core Ops, SparseCore 0:
  361.9 146.8 all-reduce.9
where the time goes:
time: 523 us; the launch traced here: 522 us
  other arithmetic  259 us (50%)
  local copies, waits for them, and re-layouts  154 us (29%)
  waiting for transfers between devices  38.5 us (7%)
  matrix products  31.6 us (6%)
  starting transfers between devices  23.2 us (4%)
  between operations  15.3 us (3%)
    scatter-add x1, other arithmetic, on_device(): jax.ops.segment_sum(d_receiver, receiver_ids, cell_count, indices_are_sor...  76.1 us
    scatter-add x1, other arithmetic, on_device(): jax.ops.segment_sum(edge_new.astype(jnp.float32), receiver_ids, cell_coun...  76 us
    scatter-add x1, other arithmetic, on_device(): jax.ops.segment_sum(d_sender, sender_ids, flat_pad.shape[0])  66.6 us
    gather x1, local copies, waits for them, and re-layouts, on_device(): sender_rows = jnp.take(flat_pad, sender_ids, axis=0)  43.7 us
    gather x1, local copies, waits for them, and re-layouts, on_device(): receiver_rows = jnp.take(own_rows, receiver_ids, axis=0)  43.3 us
    gather x1, local copies, waits for them, and re-layouts, on_device(): jnp.take(dx_node[:, latent:], receiver_ids, axis=0)  41.2 us
    psum x1, waiting for transfers between devices, reduce_flat(): return lax.psum(flat_grads, ('gx', 'gy', 'gz'))  33 us
    ppermute x6, starting transfers between devices, with_halo(): lax.ppermute(last, axis, up)  11.8 us
  transfers between devices with their start and end apart: 13, of which 2 were waited for; matrix products, arithmetic and copies ran while one was open for 28% of the time, Pallas kernels for 0%

commit v1 on v0

--- a/solution.py
+++ b/solution.py
@@ -1,7 +1,17 @@
+import functools
 import jax
 import jax.numpy as jnp
 from jax import lax
 from jax.sharding import PartitionSpec as P
+
+
+def press_counts_on(frame_in, net_axis, axis_key):
+    for j0 in (net_axis, axis_key):
+        frame_in = jax.lax.psum(frame_in, j0)
+    return frame_in
+
+
+enter_squares = functools.partial(press_counts_on, net_axis=("gy", "gz"), axis_key="gx")
 
 
 def with_halo(shard, sides, width):
@@ -40,7 +50,7 @@
 
 
 def reduce_flat(flat_grads):
-    return lax.psum(flat_grads, ("gx", "gy", "gz"))
+    return enter_squares(flat_grads)
 
 
 def on_device(

time: 523 us -> 526 us (level)
    psum x1 -> x2, waiting for transfers between devices: 33 us -> 32.6 us  [press_counts_on(): frame_in = jax.lax.psum(frame_in, j0)]
  transfers between devices with their start and end apart: 13 -> 14, of which waited for: 2 -> 3; matrix products, arithmetic and copies ran while one was open for 28% -> 28% of each run, Pallas kernels for 0% -> 0%
where the time goes in v1:
time: 526 us; the launch traced here: 523 us
  other arithmetic  260 us (49%)
  local copies, waits for them, and re-layouts  154 us (29%)
  waiting for transfers between devices  38.2 us (7%)
  matrix products  31.6 us (6%)
  starting transfers between devices  23.3 us (4%)
  between operations  15.3 us (3%)
    scatter-add x1, other arithmetic, on_device(): jax.ops.segment_sum(d_receiver, receiver_ids, cell_count, indices_are_sor...  76.1 us
    scatter-add x1, other arithmetic, on_device(): jax.ops.segment_sum(edge_new.astype(jnp.float32), receiver_ids, cell_coun...  76 us
    scatter-add x1, other arithmetic, on_device(): jax.ops.segment_sum(d_sender, sender_ids, flat_pad.shape[0])  66.6 us
    gather x1, local copies, waits for them, and re-layouts, on_device(): sender_rows = jnp.take(flat_pad, sender_ids, axis=0)  43.7 us
    gather x1, local copies, waits for them, and re-layouts, on_device(): receiver_rows = jnp.take(own_rows, receiver_ids, axis=0)  43.3 us
    gather x1, local copies, waits for them, and re-layouts, on_device(): jnp.take(dx_node[:, latent:], receiver_ids, axis=0)  41.2 us
    psum x2, waiting for transfers between devices, press_counts_on(): frame_in = jax.lax.psum(frame_in, j0)  32.6 us
    ppermute x6, starting transfers between devices, with_halo(): lax.ppermute(last, axis, up)  11.8 us
  transfers between devices with their start and end apart: 14, of which 3 were waited for; matrix products, arithmetic and copies ran while one was open for 28% of the time, Pallas kernels for 0%

profile of v1, /device:TPU:1, one launch (start us, length us, event | category | flops | bytes accessed | tf_op | source)
XLA Modules:
  0.0 523.2 jit_solution(10501172493547226681)
XLA Ops:
  10.2 3.6 collective-permute-start.4
  19.2 3.8 collective-permute-start
  28.0 43.3 %gather_fusion.1 = bf16[12288,128]{1,0:T(8,128)(2,1)} fusion(bf16[2048,128]{1,0:T(8,128)(2,1)S(1)} %bitcast.62, s32[12288]{0:T(1024)S(1)} %broadcast_clamp_fusion), kind=kCustom, calls=%fused_computation.1 | custom fusion | bytes 6340608 | tf_op jit(solution)/shard_map/jit(_take)/gather | solution.py:83
  73.8 43.7 %gather_fusion = bf16[12288,128]{1,0:T(8,128)(2,1)} fusion(bf16[3672,128]{1,0:T(8,128)(2,1)S(1)} %reshape.366, s32[12288]{0:T(1024)S(1)} %broadcast_clamp_fusion.1), kind=kCustom, calls=%fused_computation | custom fusion | bytes 6340608 | tf_op jit(solution)/shard_map/jit(_take)/gather | solution.py:82
  117.5 9.2 %broadcast_select_fusion = (bf16[12288,128]{1,0:T(8,128)(2,1)S(1)}, bf16[12288,128]{1,0:T(8,128)(2,1)S(1)}) fusion(bf16[12288,128]{1,0:T(8,128)(2,1)} %gather_fusion, pred[12288]{0:T(1024)(128)(4,1)S(1)} %compare_and_fusion, bf16[12288,128]{1,0:T(8,128)(2,1)} %gather_fusion.1, pred[12288]{0:T(1024)(128)(4,1)S(1)} %compare_and_fusion.1), kind=kLoop, calls=%fused_computation.38 | loop fusion | flops 3145728 | bytes 12607488 | tf_op jit(solution)/shard_map/jit(_take)/select_n | solution.py:82
  132.5 3.8 fusion.4
  136.3 76.0 %scatter_custom_fusion = f32[2048,128]{1,0:T(8,128)S(1)} fusion(s32[12288]{0:T(1024)S(1)} %bitcast.69, f32[12288,128]{1,0:T(8,128)} %fusion.4, f32[]{:T(128)} %constant.207.clone.1), kind=kCustom, calls=%fused_computation.83 | custom fusion | flops 1572864 | bytes 1049088 | tf_op jit(solution)/shard_map/scatter-add | solution.py:92
  215.6 41.2 %gather_fusion.2 = f32[12288,128]{1,0:T(8,128)} fusion(f32[2048,128]{1,0:T(8,128)S(1)} %get-tuple-element.81, s32[12288]{0:T(1024)S(1)} %broadcast_clamp_fusion), kind=kCustom, calls=%fused_computation.2 | custom fusion | bytes 12632064 | tf_op jit(solution)/shard_map/jit(_take)/gather | solution.py:111
  256.8 9.3 %convert_reduce_fusion = (f32[128]{0:T(128)S(1)}, bf16[12288,128]{1,0:T(8,128)(2,1)S(1)}) fusion(f32[12288,128]{1,0:T(8,128)} %gather_fusion.2, pred[12288]{0:T(1024)(128)(4,1)S(1)} %compare_and_fusion.1, bf16[1,1,1,12288,128]{4,3,2,1,0:T(8,128)(2,1)} %param.37), kind=kLoop, calls=%fused_computation.17 | loop fusion | flops 9437056 | bytes 12595712 | tf_op jit(solution)/shard_map/reduce_sum | solution.py:44
  266.1 5.4 %convolution_bitcast_fusion.2 = f32[16384]{0:T(1024)} fusion(bf16[12288,128]{1,0:T(8,128)(2,1)S(1)} %get-tuple-element.80, f32[12288,128]{1,0:T(8,128)} %copy-done.25), kind=kOutput, calls=%fused_computation.63 | convolution fusion | flops 410517504 | bytes 9502720 | tf_op jit(solution)/shard_map/dot_general | solution.py:38
  271.6 3.2 convert_reduce_fusion.1
  275.3 3.3 convolution_bitcast_fusion
  281.3 3.6 fusion.47
  284.9 3.6 fusion.49
  288.5 66.6 %scatter_custom_fusion.1 = f32[3672,128]{1,0:T(8,128)S(1)} fusion(s32[12288]{0:T(1024)} %bitcast.74, f32[12288,128]{1,0:T(8,128)} %fusion.49, f32[]{:T(128)} %constant.207.clone.1), kind=kCustom, calls=%fused_computation.81 | custom fusion | flops 1572864 | bytes 1880576 | tf_op jit(solution)/shard_map/scatter-add | solution.py:131
  361.8 3.6 collective-permute-start.10
  368.1 4.4 collective-permute-start.6
  372.5 76.1 %scatter_fusion = f32[2048,128]{1,0:T(8,128)S(1)} fusion(f32[2048,128]{1,0:T(8,128)S(1)} %get-tuple-element.82, s32[12288]{0:T(1024)S(1)} %bitcast.70, f32[12288,128]{1,0:T(8,128)} %fusion.47), kind=kCustom, calls=%fused_computation.5 | custom fusion | flops 1572864 | bytes 18923520 | tf_op jit(solution)/shard_map/scatter-add | solution.py:134
  451.4 5.6 %collective-permute-done.11 = bf16[18,34,1,128]{3,2,1,0:T(2,128)(2,1)S(1)} collective-permute-done((bf16[18,34,1,128]{3,2,1,0:T(2,128)(2,1)}, bf16[18,34,1,128]{3,2,1,0:T(2,128)(2,1)S(1)}, u32[]{:S(2)}, u32[]{:S(2)}) %collective-permute-start.11) | collective-permute-done | bytes 156704 | tf_op jit(solution)/shard_map/ppermute | solution.py:26
  457.0 3.4 fusion.30
  462.0 5.4 %all-reduce.11.cloned.1.call-done = f32[115200]{0:T(1024)} async-done(((f32[115200]{0:T(1024)}), f32[115200]{0:T(1024)}) %all-reduce.11.cloned.1.call-update) | async-done | bytes 460816 | tf_op jit(solution)/shard_map/psum | solution.py:10
  469.4 5.3 %scatter-add.58 = f32[16,32,4,128]{3,2,1,0:T(4,128)S(1)} dynamic-update-slice(f32[16,32,4,128]{3,2,1,0:T(4,128)S(1)} %fusion.44, f32[16,32,1,128]{3,2,1,0:T(1,128)S(1)} %slice_add_fusion.3, s32[]{:T(128)} %constant.208.clone.1, s32[]{:T(128)} %constant.208.clone.1, s32[]{:T(128)} %constant.208.clone.1, s32[]{:T(128)} %constant.208.clone.1) | dynamic-update-slice | bytes 524292 | tf_op jit(solution)/shard_map/scatter-add | solution.py:147
  476.8 5.3 %scatter-add.59 = f32[16,32,4,128]{3,2,1,0:T(4,128)S(1)} dynamic-update-slice(f32[16,32,4,128]{3,2,1,0:T(4,128)S(1)} %scatter-add.58, f32[16,32,1,128]{3,2,1,0:T(1,128)S(1)} %slice_add_fusion.2, s32[]{:T(128)} %constant.208.clone.1, s32[]{:T(128)} %constant.208.clone.1, s32[]{:T(128)} %constant.219.clone.1, s32[]{:T(128)} %constant.208.clone.1) | dynamic-update-slice | bytes 524292 | tf_op jit(solution)/shard_map/scatter-add | solution.py:147
  483.1 27.1 %all-reduce.13.cloned.1.call-done = f32[115200]{0:T(1024)} async-done(((f32[115200]{0:T(1024)}), f32[115200]{0:T(1024)}) %all-reduce.13.cloned.1.call-update) | async-done | bytes 460816 | tf_op jit(solution)/shard_map/psum | solution.py:10
  (128 shorter events, 51.8 us)
Async XLA Ops:
  7.2 205.2 %copy-start = (bf16[256,128]{1,0:T(8,128)(2,1)S(1)}, bf16[256,128]{1,0:T(8,128)(2,1)}, u32[]{:S(2)}) copy-start(bf16[256,128]{1,0:T(8,128)(2,1)} %param.33) | copy-start | bytes 196612
  7.2 20.8 %copy-start.2 = (bf16[16,32,4,128]{3,2,1,0:T(4,128)(2,1)S(1)}, bf16[16,32,4,128]{3,2,1,0:T(4,128)(2,1)}, u32[]{:S(2)}) copy-start(bf16[16,32,4,128]{3,2,1,0:T(4,128)(2,1)} %param.25) | copy-start | bytes 1572868
  7.2 460.2 %all-reduce.11.cloned.1.call-start = ((), (), s32[]{:S(2)}) async-start(), calls=%async_computation | async-start | bytes 925696 | tf_op jit(solution)/shard_map/psum | solution.py:10
  8.1 18.3 %collective-permute-start.1 = (bf16[16,1,4,128]{3,2,1,0:T(4,128)(2,1)S(1)}, bf16[16,1,4,128]{3,2,1,0:T(4,128)(2,1)S(1)}, u32[]{:S(2)}, u32[]{:S(2)}) collective-permute-start(bf16[16,1,4,128]{3,2,1,0:T(4,128)(2,1)S(1)} %get-tuple-element.93), channel_id=1, source_target_pairs={{0,4},{4,8},{8,12},{12,16},{16,20},{20,24},{24,28},{28,0},{1,5},{5... | collective-permute-start | bytes 49160 | tf_op jit(solution)/shard_map/ppermute | solution.py:25
  10.2 61.2 %collective-permute-start.4 = (bf16[16,1,4,128]{3,2,1,0:T(4,128)(2,1)S(1)}, bf16[16,1,4,128]{3,2,1,0:T(4,128)(2,1)S(1)}, u32[]{:S(2)}, u32[]{:S(2)}) collective-permute-start(bf16[16,1,4,128]{3,2,1,0:T(4,128)(2,1)S(1)} %get-tuple-element.94), channel_id=1, source_target_pairs={{4,0},{8,4},{12,8},{16,12},{20,16},{24,20},{28,24},{0,28},{5,1},{9... | collective-permute-start | bytes 49160 | tf_op jit(solution)/shard_map/ppermute | solution.py:26
  14.5 56.8 %collective-permute-start.2 = (bf16[1,32,4,128]{3,2,1,0:T(4,128)(2,1)S(1)}, bf16[1,32,4,128]{3,2,1,0:T(4,128)(2,1)S(1)}, u32[]{:S(2)}, u32[]{:S(2)}) collective-permute-start(bf16[1,32,4,128]{3,2,1,0:T(4,128)(2,1)S(1)} %get-tuple-element.89), channel_id=1, source_target_pairs={{0,32},{32,64},{64,96},{96,0},{1,33},{33,65},{65,97},{97,1},{2,34}... | collective-permute-start | bytes 98312 | tf_op jit(solution)/shard_map/ppermute | solution.py:25
  15.9 55.5 %collective-permute-start.3 = (bf16[1,32,4,128]{3,2,1,0:T(4,128)(2,1)S(1)}, bf16[1,32,4,128]{3,2,1,0:T(4,128)(2,1)S(1)}, u32[]{:S(2)}, u32[]{:S(2)}) collective-permute-start(bf16[1,32,4,128]{3,2,1,0:T(4,128)(2,1)S(1)} %get-tuple-element.90), channel_id=1, source_target_pairs={{32,0},{64,32},{96,64},{0,96},{33,1},{65,33},{97,65},{1,97},{34,2}... | collective-permute-start | bytes 98312 | tf_op jit(solution)/shard_map/ppermute | solution.py:26
  19.2 52.2 %collective-permute-start = (bf16[16,32,1,128]{3,2,1,0:T(2,128)(2,1)S(1)}, bf16[16,32,1,128]{3,2,1,0:T(2,128)(2,1)S(1)}, u32[]{:S(2)}, u32[]{:S(2)}) collective-permute-start(bf16[16,32,1,128]{3,2,1,0:T(2,128)(2,1)S(1)} %get-tuple-element.91), channel_id=1, source_target_pairs={{0,1},{1,2},{2,3},{3,0},{4,5},{5,6},{6,7},{7,4},{8,9},{9,10},{10,1... | collective-permute-start | bytes 393224 | tf_op jit(solution)/shard_map/ppermute | solution.py:25
  26.3 45.0 %collective-permute-start.5 = (bf16[16,32,1,128]{3,2,1,0:T(2,128)(2,1)S(1)}, bf16[16,32,1,128]{3,2,1,0:T(2,128)(2,1)S(1)}, u32[]{:S(2)}, u32[]{:S(2)}) collective-permute-start(bf16[16,32,1,128]{3,2,1,0:T(2,128)(2,1)S(1)} %get-tuple-element.92), channel_id=1, source_target_pairs={{1,0},{2,1},{3,2},{0,3},{5,4},{6,5},{7,6},{4,7},{9,8},{10,9},{11,1... | collective-permute-start | bytes 393224 | tf_op jit(solution)/shard_map/ppermute | solution.py:26
  117.5 9.3 %copy-start.12 = (bf16[384,128]{1,0:T(8,128)(2,1)S(1)}, bf16[384,128]{1,0:T(8,128)(2,1)}, u32[]{:S(2)}) copy-start(bf16[384,128]{1,0:T(8,128)(2,1)} %param.29) | copy-start | bytes 294916
  117.5 9.3 %copy-start.17 = (bf16[1,1,1,12288,128]{4,3,2,1,0:T(8,128)(2,1)S(1)}, bf16[1,1,1,12288,128]{4,3,2,1,0:T(8,128)(2,1)}, u32[]{:S(2)}) copy-start(bf16[1,1,1,12288,128]{4,3,2,1,0:T(8,128)(2,1)} %param.26) | copy-start | bytes 9437188
  117.5 9.3 %copy-start.21 = (f32[128]{0:T(128)S(1)}, f32[128]{0:T(128)}, u32[]{:S(2)}) copy-start(f32[128]{0:T(128)} %param.30) | copy-start | bytes 1540
  132.5 79.9 %copy-start.23 = (f32[128]{0:T(128)S(1)}, f32[128]{0:T(128)}, u32[]{:S(2)}) copy-start(f32[128]{0:T(128)} %param.34) | copy-start | bytes 1540
  136.3 76.6 %copy-start.8 = (bf16[16,32,4,128]{3,2,1,0:T(4,128)(2,1)S(1)}, bf16[16,32,4,128]{3,2,1,0:T(4,128)(2,1)}, u32[]{:S(2)}) copy-start(bf16[16,32,4,128]{3,2,1,0:T(4,128)(2,1)} %param.36) | copy-start | bytes 1572868
  256.8 14.7 %slice-start = ((s8[6291456]{0:T(1024)(128)(4,1)}), s8[4194304]{0:T(1024)(128)(4,1)S(1)}, s32[]{:S(2)}) async-start(s8[6291456]{0:T(1024)(128)(4,1)} %bitcast.77), calls=%async_computation.2 | async-start | bytes 8388608
  360.8 87.9 %collective-permute-start.7 = (bf16[18,1,6,128]{3,2,1,0:T(8,128)(2,1)S(1)}, bf16[18,1,6,128]{3,2,1,0:T(8,128)(2,1)S(1)}, u32[]{:S(2)}, u32[]{:S(2)}) collective-permute-start(bf16[18,1,6,128]{3,2,1,0:T(8,128)(2,1)S(1)} %get-tuple-element.87), channel_id=1, source_target_pairs={{0,4},{4,8},{8,12},{12,16},{16,20},{20,24},{24,28},{28,0},{1,5},{5... | collective-permute-start | bytes 82952 | tf_op jit(solution)/shard_map/ppermute | solution.py:25
  361.8 148.4 %all-reduce.13.cloned.1.call-start = ((), (), s32[]{:S(2)}) async-start(), calls=%async_computation.1 | async-start | bytes 925696 | tf_op jit(solution)/shard_map/psum | solution.py:10
  361.8 89.5 %collective-permute-start.10 = (bf16[18,1,6,128]{3,2,1,0:T(8,128)(2,1)S(1)}, bf16[18,1,6,128]{3,2,1,0:T(8,128)(2,1)S(1)}, u32[]{:S(2)}, u32[]{:S(2)}) collective-permute-start(bf16[18,1,6,128]{3,2,1,0:T(8,128)(2,1)S(1)} %get-tuple-element.88), channel_id=1, source_target_pairs={{4,0},{8,4},{12,8},{16,12},{20,16},{24,20},{28,24},{0,28},{5,1},{9... | collective-permute-start | bytes 82952 | tf_op jit(solution)/shard_map/ppermute | solution.py:26
  365.4 85.9 %collective-permute-start.8 = (bf16[1,34,6,128]{3,2,1,0:T(8,128)(2,1)}, bf16[1,34,6,128]{3,2,1,0:T(8,128)(2,1)}, u32[]{:S(2)}, u32[]{:S(2)}) collective-permute-start(bf16[1,34,6,128]{3,2,1,0:T(8,128)(2,1)} %get-tuple-element.83), channel_id=1, source_target_pairs={{0,32},{32,64},{64,96},{96,0},{1,33},{33,65},{65,97},{97,1},{2,34}... | collective-permute-start | bytes 156680 | tf_op jit(solution)/shard_map/ppermute | solution.py:25
  365.6 85.8 %collective-permute-start.9 = (bf16[1,34,6,128]{3,2,1,0:T(8,128)(2,1)}, bf16[1,34,6,128]{3,2,1,0:T(8,128)(2,1)}, u32[]{:S(2)}, u32[]{:S(2)}) collective-permute-start(bf16[1,34,6,128]{3,2,1,0:T(8,128)(2,1)} %get-tuple-element.84), channel_id=1, source_target_pairs={{32,0},{64,32},{96,64},{0,96},{33,1},{65,33},{97,65},{1,97},{34,2}... | collective-permute-start | bytes 156680 | tf_op jit(solution)/shard_map/ppermute | solution.py:26
  368.1 83.3 %collective-permute-start.6 = (bf16[18,34,1,128]{3,2,1,0:T(2,128)(2,1)}, bf16[18,34,1,128]{3,2,1,0:T(2,128)(2,1)}, u32[]{:S(2)}, u32[]{:S(2)}) collective-permute-start(bf16[18,34,1,128]{3,2,1,0:T(2,128)(2,1)} %get-tuple-element.85), channel_id=1, source_target_pairs={{0,1},{1,2},{2,3},{3,0},{4,5},{5,6},{6,7},{7,4},{8,9},{9,10},{10,1... | collective-permute-start | bytes 470024 | tf_op jit(solution)/shard_map/ppermute | solution.py:25
  448.7 8.3 %collective-permute-start.11 = (bf16[18,34,1,128]{3,2,1,0:T(2,128)(2,1)}, bf16[18,34,1,128]{3,2,1,0:T(2,128)(2,1)S(1)}, u32[]{:S(2)}, u32[]{:S(2)}) collective-permute-start(bf16[18,34,1,128]{3,2,1,0:T(2,128)(2,1)} %get-tuple-element.86), channel_id=1, source_target_pairs={{1,0},{2,1},{3,2},{0,3},{5,4},{6,5},{7,6},{4,7},{9,8},{10,9},{11,1... | collective-permute-start | bytes 470024 | tf_op jit(solution)/shard_map/ppermute | solution.py:26
  449.3 7.7 %copy-start.16 = (bf16[18,1,6,128]{3,2,1,0:T(8,128)(2,1)S(1)}, bf16[18,1,6,128]{3,2,1,0:T(8,128)(2,1)}, u32[]{:S(2)}) copy-start(bf16[18,1,6,128]{3,2,1,0:T(8,128)(2,1)} %copy-done.15) | copy-start | bytes 82948
  467.5 48.9 %copy-start.1 = (bf16[256,128]{1,0:T(8,128)(2,1)S(1)}, bf16[256,128]{1,0:T(8,128)(2,1)}, u32[]{:S(2)}) copy-start(bf16[256,128]{1,0:T(8,128)(2,1)} %param.33) | copy-start | bytes 196612
  (18 other events, 60.3 us)
Sparse Core Ops, SparseCore 0:
  361.9 105.4 all-reduce.10
  469.8 40.3 all-reduce.12
